TPU v7x, 32 devices: a whole 2x2x4 slice. The times are simulated.
32 devices in a mesh: batch: 8 (over y, x, core), shard: 4 (over z).
Axes of the slice: x: 2, y: 2, z: 4, core: 2. Of those that a mesh axis runs over, the one named last changes fastest.
Arguments:
- particles: float32 [8192, 1024], P(('batch', 'shard')), may hold values from -48 to 48
- batch_of: int32 [2, 8192], P(None, ('batch', 'shard')), may hold values from 0 to 7, as said below
- mixture_means: float32 [16, 1024], replicated, may hold values from -3 to 3
- log_weights: float32 [16], replicated, may hold values from -2 to 2
Outputs:
- moved: float32 [8192, 1024], P(('batch', 'shard'))
Inputs may be any that keep to these rules, and one draw needn't show every extreme that they name: `batch_of`: in each iteration, the 256 particles of one device hold every batch number equally often, 256 / 8 times each.
All inputs are finite; a program needn't handle non-finite values.
Results may differ from a plain program's by a relative error of at most 0.00011.
Values sent between devices are 32-bit elements; how exact they have to be, the bound alone decides.
A program may use at most 64 MiB of HBM per device.

v0:
```python
import functools

import jax
import jax.numpy as jnp
from jax import lax
from jax.experimental import pallas as pl
from jax.experimental.pallas import tpu as pltpu
from jax.sharding import PartitionSpec as P

variance = 4.0
step_size = 32.0
MESH = pl.DeviceIdType.MESH


def split(a):
    high = a.astype(jnp.bfloat16)
    return high, (a - high.astype(jnp.float32)).astype(jnp.bfloat16)


def dot3(a, b, contract):
    dims = (contract, ((), ()))
    one = functools.partial(lax.dot_general, dimension_numbers=dims, preferred_element_type=jnp.float32)
    return one(a[0], b[0]) + (one(a[0], b[1]) + one(a[1], b[0]))


def step_kernel(
    groups,
    shards,
    rows_ref,
    means_ref,
    logw_ref,
    out_ref,
    pool,
    lhs_high,
    lhs_low,
    own_sq,
    acc,
    acc_w,
    acc_k,
    moved,
    own_sem,
    a_send,
    a_recv,
    x_send,
    x_recv,
    c_send,
    c_recv,
    r_send,
    r_recv,
):
    count, width = rows_ref.shape
    chunk = count // groups
    members = shards
    pairs = members // 2
    components = means_ref.shape[0]
    b = lax.axis_index("batch")
    s = lax.axis_index("shard")
    q, t = b // members, b % members
    x, c = t // 2, t % 2
    g = q * shards + s

    def piece(index):
        return pl.ds(pl.multiple_of(index * chunk, chunk), chunk)

    def place(group):
        return (group // shards) * members + t, group % shards

    def mate(j, other):
        return q * members + lax.rem(x + j, pairs) * 2 + (1 - c if other else c), s

    barrier = pltpu.get_barrier_semaphore()
    targets = [place(lax.rem(g + k, groups)) for k in range(1, groups)]
    targets += [mate(j, False) for j in range(1, pairs)] + [mate(0, True)]
    for target in targets:
        pl.semaphore_signal(barrier, inc=1, device_id=target, device_id_type=MESH)
    pl.semaphore_wait(barrier, len(targets))

    own = pltpu.make_async_copy(rows_ref.at[piece(g)], pool.at[t, piece(g)], own_sem.at[0])
    own.start()
    sends = [own]
    for k in range(1, groups):
        to = lax.rem(g + k, groups)
        sends.append(
            pltpu.make_async_remote_copy(
                src_ref=rows_ref.at[piece(to)],
                dst_ref=pool.at[t, piece(g)],
                send_sem=a_send.at[k],
                recv_sem=a_recv.at[k],
                device_id=place(to),
                device_id_type=MESH,
            )
        )
        sends[-1].start()

    def pass_on(j, k, other):
        source = lax.rem(g + groups - k, groups)
        block = lax.rem(x + pairs - (j if other else 0), pairs) * 2 + c
        sem = (c_send, c_recv) if other else (x_send, x_recv)
        copy = pltpu.make_async_remote_copy(
            src_ref=pool.at[block, piece(source)],
            dst_ref=pool.at[block, piece(source)],
            send_sem=sem[0].at[j, k],
            recv_sem=sem[1].at[j, k],
            device_id=mate(0, True) if other else mate(j, False),
            device_id_type=MESH,
        )
        copy.start()
        return copy

    across, inside = {}, {}
    for k in range(groups):
        if k == 0:
            own.wait()
        else:
            sends[k].wait_recv()
        for j in range(1, pairs):
            across[j, k] = pass_on(j, k, False)
        inside[0, k] = pass_on(0, k, True)
        if k >= 2:
            for j in range(1, pairs):
                across[j, k - 2].wait_recv()
                inside[j, k - 2] = pass_on(j, k - 2, True)

    means = means_ref[...]
    mean_parts = split(means)
    mean_sq = jnp.sum(means * means, axis=1, keepdims=True)
    own_rows = pool[t]
    own_parts = split(own_rows)
    lhs_high[0:count, :] = own_parts[0]
    lhs_low[0:count, :] = own_parts[1]
    lhs_high[count:, :] = mean_parts[0]
    lhs_low[count:, :] = mean_parts[1]
    own_sq[...] = jnp.sum(own_rows * own_rows, axis=1, keepdims=True)

    def process(block, first):
        points = pool[block]
        parts = split(points)
        sq = jnp.sum(points * points, axis=1, keepdims=True)
        sq_row = jnp.transpose(jnp.broadcast_to(sq, (count, 128)))[0:1, :]
        crossed = dot3((lhs_high[...], lhs_low[...]), parts, ((1,), (1,)))
        kernel = jnp.exp(-(own_sq[...] + sq_row - 2.0 * crossed[:count]) * (2.0 / width))
        logits = logw_ref[...] - (sq_row - 2.0 * crossed[count:] + mean_sq) / (2.0 * variance)
        weights = jnp.exp(logits - jnp.max(logits, axis=0, keepdims=True))
        weights = weights / jnp.sum(weights, axis=0, keepdims=True)
        kernel_parts = split(kernel)
        point = dot3(kernel_parts, parts, ((1,), (0,)))
        mixed = dot3(kernel_parts, split(weights), ((1,), (1,)))
        total = jnp.sum(kernel, axis=1, keepdims=True)
        if first:
            acc[...] = point
            acc_w[...] = mixed
            acc_k[...] = total
        else:
            acc[...] += point
            acc_w[...] += mixed
            acc_k[...] += total

    process(t, True)

    for k in range(max(groups - 2, 0), groups):
        for j in range(1, pairs):
            across[j, k].wait_recv()
            inside[j, k] = pass_on(j, k, True)
    for j in range(pairs):
        for k in range(groups):
            inside[j, k].wait_recv()

    def rest(i, carry):
        j, h = i // 2, i % 2
        process(lax.rem(x + pairs - j, pairs) * 2 + lax.rem(c + h, 2), False)
        return carry

    lax.fori_loop(1, members, rest, 0)

    size = count * members
    scale = 4.0 / width
    pulled = dot3(split(acc_w[...]), mean_parts, ((1,), (0,)))
    drift = (pulled - acc[...]) / variance + scale * (pool[t] * acc_k[...] - acc[...])
    moved[...] = pool[t] + (step_size / size) * drift

    home = pltpu.make_async_copy(moved.at[piece(g)], out_ref.at[piece(g)], own_sem.at[1])
    back = [home]
    for k in range(1, groups):
        to = lax.rem(g + k, groups)
        back.append(
            pltpu.make_async_remote_copy(
                src_ref=moved.at[piece(to)],
                dst_ref=out_ref.at[piece(g)],
                send_sem=r_send.at[k],
                recv_sem=r_recv.at[k],
                device_id=place(to),
                device_id_type=MESH,
            )
        )
        back[-1].start()
    home.start()
    for copy in sends[1:]:
        copy.wait_send()
    for copy in across.values():
        copy.wait_send()
    for copy in inside.values():
        copy.wait_send()
    home.wait()
    for copy in back[1:]:
        copy.wait()


def step(rows, means, logw, groups, shards):
    count, width = rows.shape
    components = means.shape[0]
    pairs = shards // 2
    dma = pltpu.SemaphoreType.DMA
    return pl.pallas_call(
        functools.partial(step_kernel, groups, shards),
        out_shape=jax.ShapeDtypeStruct((count, width), jnp.float32),
        in_specs=[pl.BlockSpec(memory_space=pltpu.VMEM)] * 3,
        out_specs=pl.BlockSpec(memory_space=pltpu.VMEM),
        scratch_shapes=[
            pltpu.VMEM((shards, count, width), jnp.float32),
            pltpu.VMEM((count + components, width), jnp.bfloat16),
            pltpu.VMEM((count + components, width), jnp.bfloat16),
            pltpu.VMEM((count, 1), jnp.float32),
            pltpu.VMEM((count, width), jnp.float32),
            pltpu.VMEM((count, components), jnp.float32),
            pltpu.VMEM((count, 1), jnp.float32),
            pltpu.VMEM((count, width), jnp.float32),
            dma((2,)),
            dma((groups,)),
            dma((groups,)),
            dma((pairs, groups)),
            dma((pairs, groups)),
            dma((pairs, groups)),
            dma((pairs, groups)),
            dma((groups,)),
            dma((groups,)),
        ],
        compiler_params=pltpu.CompilerParams(
            collective_id=0, has_side_effects=True, vmem_limit_bytes=48 * 1024 * 1024
        ),
    )(rows, means, logw)


def permutation(batch, groups):
    count = batch.shape[0]
    chunk = count // groups
    index = jnp.arange(count, dtype=jnp.int32)
    same = (batch[:, None] == batch[None, :]) & (index[:, None] < index[None, :])
    spot = batch * chunk + jnp.sum(same.astype(jnp.int32), axis=0)
    return (index[:, None] == spot[None, :]).astype(jnp.float32)


def apply(matrix, rows, transposed=False):
    dims = (((0,), (0,)) if transposed else ((1,), (0,)), ((), ()))
    return lax.dot_general(
        matrix, rows, dims, precision=lax.Precision.HIGHEST, preferred_element_type=jnp.float32
    )


def body(particles, batch_of, mixture_means, log_weights):
    groups = lax.axis_size("batch")
    shards = lax.axis_size("shard")
    logw = log_weights[:, None]
    current = particles
    previous = None
    for iteration in range(batch_of.shape[0]):
        order = permutation(batch_of[iteration], groups)
        if previous is None:
            current = apply(order, current)
        else:
            both = lax.dot_general(
                order.astype(jnp.bfloat16),
                previous.astype(jnp.bfloat16),
                (((1,), (1,)), ((), ())),
                preferred_element_type=jnp.float32,
            )
            current = apply(both, current)
        current = step(current, mixture_means, logw, groups, shards)
        previous = order
    return apply(previous, current, transposed=True)


def solution(mesh):
    placed = (P(("batch", "shard"), None), P(None, ("batch", "shard")), P(), P())
    return jax.shard_map(
        body, mesh=mesh, in_specs=placed, out_specs=P(("batch", "shard"), None), check_vma=False
    )
```

profile of v0, /device:TPU:9, one launch (start us, length us, event | category | flops | bytes accessed | tf_op | source)
XLA Modules:
  0.0 144.4 jit_solution(15287855371798308009)
XLA Ops:
  0.0 0.0 copy-start
  0.0 0.8 fusion.9
  0.8 0.1 convert_reduce_fusion.1
  0.9 0.0 copy-start.2
  0.9 0.1 convert_reduce_fusion
  1.0 0.6 copy-done.2
  1.6 0.0 copy-start.3
  1.6 0.7 copy-done.3
  2.3 0.1 copy.7.logw_ref
  2.3 0.2 fusion.4
  2.6 0.0 copy-done
  2.6 0.0 copy-start.1
  2.6 0.7 fusion.rows_ref
  3.3 0.1 copy-done.1
  3.4 69.0 %shard_map.46 = f32[256,1024]{1,0:T(8,128)S(1)} custom-call(f32[256,1024]{1,0:T(8,128)S(1)} %fusion.rows_ref, f32[16,1024]{1,0:T(8,128)S(1)} %copy-done.1, f32[16,1]{1,0:T(8,128)S(1)} %copy.7.logw_ref), custom_call_target="tpu_custom_call" | custom-call | tf_op jit(solution)/shard_map/pallas_call | solution.py:213
  72.5 1.0 fusion.10.rows_ref
  73.5 69.2 %shard_map.47 = f32[256,1024]{1,0:T(8,128)S(1)} custom-call(f32[256,1024]{1,0:T(8,128)S(1)} %fusion.10.rows_ref, f32[16,1024]{1,0:T(8,128)S(1)} %copy-done.1, f32[16,1]{1,0:T(8,128)S(1)} %copy.7.logw_ref), custom_call_target="tpu_custom_call" | custom-call | tf_op jit(solution)/shard_map/pallas_call | solution.py:213
  142.7 1.7 %fusion.3 = f32[256,1024]{1,0:T(8,128)} fusion(f32[256,1024]{1,0:T(8,128)S(1)} %shard_map.47, s32[256]{0:T(256)S(1)} %bitcast.12), kind=kOutput, calls=%fused_computation.10 | convolution fusion | flops 805371904 | bytes 2098176 | tf_op jit(solution)/shard_map/dot_general | solution.py:254
  (1 shorter events, 0.0 us)
Async XLA Ops:
  0.0 2.6 %copy-start = (f32[256,1024]{1,0:T(8,128)S(1)}, f32[256,1024]{1,0:T(8,128)}, u32[]{:S(2)}) copy-start(f32[256,1024]{1,0:T(8,128)} %param.4) | copy-start | bytes 3145732
  0.9 0.7 copy-start.2
  1.6 0.7 copy-start.3
  2.6 0.8 copy-start.1
where the time goes:
time: 145 us; the launch traced here: 144 us
  Pallas kernels  138 us (95%)
  matrix products  3.66 us (3%)
  local copies, waits for them, and re-layouts  2.23 us (2%)
    pallas_call x2, Pallas kernels, step(): pl.pallas_call(functools.partial(step_kernel, groups, shards), out_shape=...  138 us
    dot_general x3, matrix products, apply(): lax.dot_general(matrix, rows, dims, precision=lax.Precision.HIGHEST, pref...  3.41 us

commit v1 on v0

--- a/solution.py
+++ b/solution.py
@@ -31,12 +31,15 @@
     logw_ref,
     out_ref,
     pool,
+    mine,
     lhs_high,
     lhs_low,
     own_sq,
     acc,
     acc_w,
     acc_k,
+    late_high,
+    late_low,
     moved,
     own_sem,
     a_send,
@@ -50,26 +53,50 @@
 ):
     count, width = rows_ref.shape
     chunk = count // groups
+    half = count // 2
     members = shards
     pairs = members // 2
-    components = means_ref.shape[0]
+    wide = groups // shards
+    near = shards // 2
     b = lax.axis_index("batch")
     s = lax.axis_index("shard")
     q, t = b // members, b % members
     x, c = t // 2, t % 2
     g = q * shards + s
-
-    def piece(index):
-        return pl.ds(pl.multiple_of(index * chunk, chunk), chunk)
-
-    def place(group):
-        return (group // shards) * members + t, group % shards
+    h, l = s // near, s % near
+
+    def piece(index, start=0, rows=chunk):
+        return pl.ds(pl.multiple_of(index * chunk + start, 8), rows)
+
+    def group(step, sign):
+        far, i, dq = step
+        side = 1 - h if far else h
+        column = side * near + lax.rem(l + near + sign * i, near)
+        return lax.rem(q + wide + sign * dq, wide) * shards + column
+
+    def place(index):
+        return (index // shards) * members + t, index % shards
 
     def mate(j, other):
         return q * members + lax.rem(x + j, pairs) * 2 + (1 - c if other else c), s
 
+    self_step = (0, 0, 0)
+    same = [(0, 0, dq) for dq in range(1, wide)]
+    close = [(0, i, dq) for i in range(1, near) for dq in range(wide)]
+    far = [(1, i, dq) for i in range(near) for dq in range(wide)]
+    mixed_order = []
+    for n in range(max(len(far), len(close))):
+        mixed_order += far[n : n + 1] + close[n : n + 1]
+    steps = [self_step] + same + mixed_order
+    items = []
+    for n, at in enumerate(steps):
+        if n >= groups - 2:
+            items += [(at, 0, chunk // 2), (at, chunk // 2, chunk // 2)]
+        else:
+            items.append((at, 0, chunk))
+
     barrier = pltpu.get_barrier_semaphore()
-    targets = [place(lax.rem(g + k, groups)) for k in range(1, groups)]
+    targets = [place(group(at, 1)) for at in steps[1:]]
     targets += [mate(j, False) for j in range(1, pairs)] + [mate(0, True)]
     for target in targets:
         pl.semaphore_signal(barrier, inc=1, device_id=target, device_id_type=MESH)
@@ -78,29 +105,30 @@
     own = pltpu.make_async_copy(rows_ref.at[piece(g)], pool.at[t, piece(g)], own_sem.at[0])
     own.start()
     sends = [own]
-    for k in range(1, groups):
-        to = lax.rem(g + k, groups)
+    for n, (at, start, rows) in enumerate(items[1:], 1):
+        to = group(at, 1)
         sends.append(
             pltpu.make_async_remote_copy(
-                src_ref=rows_ref.at[piece(to)],
-                dst_ref=pool.at[t, piece(g)],
-                send_sem=a_send.at[k],
-                recv_sem=a_recv.at[k],
+                src_ref=rows_ref.at[piece(to, start, rows)],
+                dst_ref=pool.at[t, piece(g, start, rows)],
+                send_sem=a_send.at[n],
+                recv_sem=a_recv.at[n],
                 device_id=place(to),
                 device_id_type=MESH,
             )
         )
         sends[-1].start()
 
-    def pass_on(j, k, other):
-        source = lax.rem(g + groups - k, groups)
+    def pass_on(j, n, other):
+        at, start, rows = items[n]
+        source = piece(group(at, -1), start, rows)
         block = lax.rem(x + pairs - (j if other else 0), pairs) * 2 + c
         sem = (c_send, c_recv) if other else (x_send, x_recv)
         copy = pltpu.make_async_remote_copy(
-            src_ref=pool.at[block, piece(source)],
-            dst_ref=pool.at[block, piece(source)],
-            send_sem=sem[0].at[j, k],
-            recv_sem=sem[1].at[j, k],
+            src_ref=pool.at[block, source],
+            dst_ref=pool.at[block, source],
+            send_sem=sem[0].at[j, n],
+            recv_sem=sem[1].at[j, n],
             device_id=mate(0, True) if other else mate(j, False),
             device_id_type=MESH,
         )
@@ -108,29 +136,33 @@
         return copy
 
     across, inside = {}, {}
-    for k in range(groups):
-        if k == 0:
+    for n in range(len(items)):
+        if n == 0:
             own.wait()
         else:
-            sends[k].wait_recv()
+            sends[n].wait_recv()
         for j in range(1, pairs):
-            across[j, k] = pass_on(j, k, False)
-        inside[0, k] = pass_on(0, k, True)
-        if k >= 2:
+            across[j, n] = pass_on(j, n, False)
+        inside[0, n] = pass_on(0, n, True)
+        if n >= 2:
             for j in range(1, pairs):
-                across[j, k - 2].wait_recv()
-                inside[j, k - 2] = pass_on(j, k - 2, True)
+                across[j, n - 2].wait_recv()
+                inside[j, n - 2] = pass_on(j, n - 2, True)
 
     means = means_ref[...]
     mean_parts = split(means)
     mean_sq = jnp.sum(means * means, axis=1, keepdims=True)
-    own_rows = pool[t]
-    own_parts = split(own_rows)
-    lhs_high[0:count, :] = own_parts[0]
-    lhs_low[0:count, :] = own_parts[1]
+    back_order = far + close + same + [self_step]
+    for n, at in enumerate(back_order):
+        block = pool[t, piece(group(at, 1))]
+        high, low = split(block)
+        spot = slice(n * chunk, (n + 1) * chunk)
+        mine[spot, :] = block
+        lhs_high[spot, :] = high
+        lhs_low[spot, :] = low
+        own_sq[spot, :] = jnp.sum(block * block, axis=1, keepdims=True)
     lhs_high[count:, :] = mean_parts[0]
     lhs_low[count:, :] = mean_parts[1]
-    own_sq[...] = jnp.sum(own_rows * own_rows, axis=1, keepdims=True)
 
     def process(block, first):
         points = pool[block]
@@ -142,9 +174,11 @@
         logits = logw_ref[...] - (sq_row - 2.0 * crossed[count:] + mean_sq) / (2.0 * variance)
         weights = jnp.exp(logits - jnp.max(logits, axis=0, keepdims=True))
         weights = weights / jnp.sum(weights, axis=0, keepdims=True)
-        kernel_parts = split(kernel)
-        point = dot3(kernel_parts, parts, ((1,), (0,)))
-        mixed = dot3(kernel_parts, split(weights), ((1,), (1,)))
+        high, low = split(kernel)
+        late_high[block] = high[half:]
+        late_low[block] = low[half:]
+        point = dot3((high[:half], low[:half]), parts, ((1,), (0,)))
+        mixed = dot3((high, low), split(weights), ((1,), (1,)))
         total = jnp.sum(kernel, axis=1, keepdims=True)
         if first:
             acc[...] = point
@@ -157,51 +191,65 @@
 
     process(t, True)
 
-    for k in range(max(groups - 2, 0), groups):
+    for n in range(len(items) - 2, len(items)):
         for j in range(1, pairs):
-            across[j, k].wait_recv()
-            inside[j, k] = pass_on(j, k, True)
-    for j in range(pairs):
-        for k in range(groups):
-            inside[j, k].wait_recv()
+            across[j, n].wait_recv()
+            inside[j, n] = pass_on(j, n, True)
+    for copy in inside.values():
+        copy.wait_recv()
 
     def rest(i, carry):
-        j, h = i // 2, i % 2
-        process(lax.rem(x + pairs - j, pairs) * 2 + lax.rem(c + h, 2), False)
+        j, e = i // 2, i % 2
+        process(lax.rem(x + pairs - j, pairs) * 2 + lax.rem(c + e, 2), False)
         return carry
 
     lax.fori_loop(1, members, rest, 0)
 
     size = count * members
     scale = 4.0 / width
-    pulled = dot3(split(acc_w[...]), mean_parts, ((1,), (0,)))
-    drift = (pulled - acc[...]) / variance + scale * (pool[t] * acc_k[...] - acc[...])
-    moved[...] = pool[t] + (step_size / size) * drift
-
-    home = pltpu.make_async_copy(moved.at[piece(g)], out_ref.at[piece(g)], own_sem.at[1])
-    back = [home]
-    for k in range(1, groups):
-        to = lax.rem(g + k, groups)
-        back.append(
-            pltpu.make_async_remote_copy(
-                src_ref=moved.at[piece(to)],
-                dst_ref=out_ref.at[piece(g)],
-                send_sem=r_send.at[k],
-                recv_sem=r_recv.at[k],
-                device_id=place(to),
-                device_id_type=MESH,
-            )
-        )
-        back[-1].start()
-    home.start()
+    back = []
+
+    def finish(first):
+        span = slice(first, first + half)
+        pulled = dot3(split(acc_w[span, :]), mean_parts, ((1,), (0,)))
+        rows = mine[span, :]
+        drift = (pulled - acc[...]) / variance + scale * (rows * acc_k[span, :] - acc[...])
+        moved[span, :] = rows + (step_size / size) * drift
+        for n in range(first // chunk, (first + half) // chunk):
+            spot = slice(n * chunk, (n + 1) * chunk)
+            to = group(back_order[n], 1)
+            if n == groups - 1:
+                copy = pltpu.make_async_copy(moved.at[spot], out_ref.at[piece(g)], own_sem.at[1])
+            else:
+                copy = pltpu.make_async_remote_copy(
+                    src_ref=moved.at[spot],
+                    dst_ref=out_ref.at[piece(g)],
+                    send_sem=r_send.at[n],
+                    recv_sem=r_recv.at[n],
+                    device_id=place(to),
+                    device_id_type=MESH,
+                )
+            copy.start()
+            back.append(copy)
+
+    finish(0)
+
+    def later(block, carry):
+        point = dot3((late_high[block], late_low[block]), split(pool[block]), ((1,), (0,)))
+        acc[...] += point
+        return carry
+
+    acc[...] = jnp.zeros_like(acc)
+    lax.fori_loop(0, members, later, 0)
+    finish(half)
+
     for copy in sends[1:]:
         copy.wait_send()
     for copy in across.values():
         copy.wait_send()
     for copy in inside.values():
         copy.wait_send()
-    home.wait()
-    for copy in back[1:]:
+    for copy in back:
         copy.wait()
 
 
@@ -217,20 +265,23 @@
         out_specs=pl.BlockSpec(memory_space=pltpu.VMEM),
         scratch_shapes=[
             pltpu.VMEM((shards, count, width), jnp.float32),
+            pltpu.VMEM((count, width), jnp.float32),
             pltpu.VMEM((count + components, width), jnp.bfloat16),
             pltpu.VMEM((count + components, width), jnp.bfloat16),
             pltpu.VMEM((count, 1), jnp.float32),
-            pltpu.VMEM((count, width), jnp.float32),
+            pltpu.VMEM((count // 2, width), jnp.float32),
             pltpu.VMEM((count, components), jnp.float32),
             pltpu.VMEM((count, 1), jnp.float32),
+            pltpu.VMEM((shards, count // 2, count), jnp.bfloat16),
+            pltpu.VMEM((shards, count // 2, count), jnp.bfloat16),
             pltpu.VMEM((count, width), jnp.float32),
             dma((2,)),
-            dma((groups,)),
-            dma((groups,)),
-            dma((pairs, groups)),
-            dma((pairs, groups)),
-            dma((pairs, groups)),
-            dma((pairs, groups)),
+            dma((groups + 2,)),
+            dma((groups + 2,)),
+            dma((pairs, groups + 2)),
+            dma((pairs, groups + 2)),
+            dma((pairs, groups + 2)),
+            dma((pairs, groups + 2)),
             dma((groups,)),
             dma((groups,)),
         ],

time: 145 us -> 132 us (0.910)
  Pallas kernels: 138 us -> 125 us
    pallas_call x2, Pallas kernels: 138 us -> 125 us  [step(): pl.pallas_call(functools.partial(step_kernel, groups, shards), out_shape=...]
where the time goes in v1:
time: 132 us
  Pallas kernels  125 us (95%)
  matrix products  3.66 us (3%)
  local copies, waits for them, and re-layouts  2.23 us (2%)
    pallas_call x2, Pallas kernels, step(): pl.pallas_call(functools.partial(step_kernel, groups, shards), out_shape=...  125 us
    dot_general x3, matrix products, apply(): lax.dot_general(matrix, rows, dims, precision=lax.Precision.HIGHEST, pref...  3.41 us

profile of v1, /device:TPU:9, one launch (start us, length us, event | category | flops | bytes accessed | tf_op | source)
XLA Modules:
  0.0 131.5 jit_solution(14754163323513596812)
XLA Ops:
  0.0 0.0 copy-start
  0.0 0.8 fusion.9
  0.8 0.1 convert_reduce_fusion.1
  0.9 0.0 copy-start.2
  0.9 0.1 convert_reduce_fusion
  1.0 0.6 copy-done.2
  1.6 0.0 copy-start.3
  1.6 0.7 copy-done.3
  2.3 0.1 copy.7.logw_ref
  2.3 0.2 fusion.4
  2.6 0.0 copy-done
  2.6 0.0 copy-start.1
  2.6 0.7 fusion.rows_ref
  3.3 0.1 copy-done.1
  3.4 63.6 %shard_map.46 = f32[256,1024]{1,0:T(8,128)S(1)} custom-call(f32[256,1024]{1,0:T(8,128)S(1)} %fusion.rows_ref, f32[16,1024]{1,0:T(8,128)S(1)} %copy-done.1, f32[16,1]{1,0:T(8,128)S(1)} %copy.7.logw_ref), custom_call_target="tpu_custom_call" | custom-call | tf_op jit(solution)/shard_map/pallas_call | solution.py:261
  67.1 1.0 fusion.10.rows_ref
  68.1 61.7 %shard_map.47 = f32[256,1024]{1,0:T(8,128)S(1)} custom-call(f32[256,1024]{1,0:T(8,128)S(1)} %fusion.10.rows_ref, f32[16,1024]{1,0:T(8,128)S(1)} %copy-done.1, f32[16,1]{1,0:T(8,128)S(1)} %copy.7.logw_ref), custom_call_target="tpu_custom_call" | custom-call | tf_op jit(solution)/shard_map/pallas_call | solution.py:261
  129.8 1.7 %fusion.3 = f32[256,1024]{1,0:T(8,128)} fusion(f32[256,1024]{1,0:T(8,128)S(1)} %shard_map.47, s32[256]{0:T(256)S(1)} %bitcast.12), kind=kOutput, calls=%fused_computation.10 | convolution fusion | flops 805371904 | bytes 2098176 | tf_op jit(solution)/shard_map/dot_general | solution.py:305
  (1 shorter events, 0.0 us)
Async XLA Ops:
  0.0 2.6 %copy-start = (f32[256,1024]{1,0:T(8,128)S(1)}, f32[256,1024]{1,0:T(8,128)}, u32[]{:S(2)}) copy-start(f32[256,1024]{1,0:T(8,128)} %param.4) | copy-start | bytes 3145732
  0.9 0.7 copy-start.2
  1.6 0.7 copy-start.3
  2.6 0.8 copy-start.1

commit v2 on v1

--- a/solution.py
+++ b/solution.py
@@ -38,8 +38,7 @@
     acc,
     acc_w,
     acc_k,
-    late_high,
-    late_low,
+    mix,
     moved,
     own_sem,
     a_send,
@@ -54,6 +53,7 @@
     count, width = rows_ref.shape
     chunk = count // groups
     half = count // 2
+    components = means_ref.shape[0]
     members = shards
     pairs = members // 2
     wide = groups // shards
@@ -157,28 +157,34 @@
         block = pool[t, piece(group(at, 1))]
         high, low = split(block)
         spot = slice(n * chunk, (n + 1) * chunk)
+        shift = 0 if n < groups // 2 else components
+        left = slice(n * chunk + shift, (n + 1) * chunk + shift)
         mine[spot, :] = block
-        lhs_high[spot, :] = high
-        lhs_low[spot, :] = low
+        lhs_high[left, :] = high
+        lhs_low[left, :] = low
         own_sq[spot, :] = jnp.sum(block * block, axis=1, keepdims=True)
-    lhs_high[count:, :] = mean_parts[0]
-    lhs_low[count:, :] = mean_parts[1]
-
-    def process(block, first):
+    lhs_high[half : half + components, :] = mean_parts[0]
+    lhs_low[half : half + components, :] = mean_parts[1]
+
+    def process(block, late, first=False):
         points = pool[block]
         parts = split(points)
         sq = jnp.sum(points * points, axis=1, keepdims=True)
         sq_row = jnp.transpose(jnp.broadcast_to(sq, (count, 128)))[0:1, :]
-        crossed = dot3((lhs_high[...], lhs_low[...]), parts, ((1,), (1,)))
-        kernel = jnp.exp(-(own_sq[...] + sq_row - 2.0 * crossed[:count]) * (2.0 / width))
-        logits = logw_ref[...] - (sq_row - 2.0 * crossed[count:] + mean_sq) / (2.0 * variance)
-        weights = jnp.exp(logits - jnp.max(logits, axis=0, keepdims=True))
-        weights = weights / jnp.sum(weights, axis=0, keepdims=True)
-        high, low = split(kernel)
-        late_high[block] = high[half:]
-        late_low[block] = low[half:]
-        point = dot3((high[:half], low[:half]), parts, ((1,), (0,)))
-        mixed = dot3((high, low), split(weights), ((1,), (1,)))
+        span = slice(half, count) if late else slice(0, half)
+        left = slice(half + components, None) if late else slice(0, half + components)
+        crossed = dot3((lhs_high[left, :], lhs_low[left, :]), parts, ((1,), (1,)))
+        kernel = jnp.exp(-(own_sq[span, :] + sq_row - 2.0 * crossed[:half]) * (2.0 / width))
+        if late:
+            weights = mix[block]
+        else:
+            logits = logw_ref[...] - (sq_row - 2.0 * crossed[half:] + mean_sq) / (2.0 * variance)
+            weights = jnp.exp(logits - jnp.max(logits, axis=0, keepdims=True))
+            weights = weights / jnp.sum(weights, axis=0, keepdims=True)
+            mix[block] = weights
+        kernel_parts = split(kernel)
+        point = dot3(kernel_parts, parts, ((1,), (0,)))
+        mixed = dot3(kernel_parts, split(weights), ((1,), (1,)))
         total = jnp.sum(kernel, axis=1, keepdims=True)
         if first:
             acc[...] = point
@@ -189,7 +195,7 @@
             acc_w[...] += mixed
             acc_k[...] += total
 
-    process(t, True)
+    process(t, False, True)
 
     for n in range(len(items) - 2, len(items)):
         for j in range(1, pairs):
@@ -211,9 +217,9 @@
 
     def finish(first):
         span = slice(first, first + half)
-        pulled = dot3(split(acc_w[span, :]), mean_parts, ((1,), (0,)))
+        pulled = dot3(split(acc_w[...]), mean_parts, ((1,), (0,)))
         rows = mine[span, :]
-        drift = (pulled - acc[...]) / variance + scale * (rows * acc_k[span, :] - acc[...])
+        drift = (pulled - acc[...]) / variance + scale * (rows * acc_k[...] - acc[...])
         moved[span, :] = rows + (step_size / size) * drift
         for n in range(first // chunk, (first + half) // chunk):
             spot = slice(n * chunk, (n + 1) * chunk)
@@ -235,11 +241,12 @@
     finish(0)
 
     def later(block, carry):
-        point = dot3((late_high[block], late_low[block]), split(pool[block]), ((1,), (0,)))
-        acc[...] += point
+        process(block, True)
         return carry
 
     acc[...] = jnp.zeros_like(acc)
+    acc_w[...] = jnp.zeros_like(acc_w)
+    acc_k[...] = jnp.zeros_like(acc_k)
     lax.fori_loop(0, members, later, 0)
     finish(half)
 
@@ -270,10 +277,9 @@
             pltpu.VMEM((count + components, width), jnp.bfloat16),
             pltpu.VMEM((count, 1), jnp.float32),
             pltpu.VMEM((count // 2, width), jnp.float32),
-            pltpu.VMEM((count, components), jnp.float32),
-            pltpu.VMEM((count, 1), jnp.float32),
-            pltpu.VMEM((shards, count // 2, count), jnp.bfloat16),
-            pltpu.VMEM((shards, count // 2, count), jnp.bfloat16),
+            pltpu.VMEM((count // 2, components), jnp.float32),
+            pltpu.VMEM((count // 2, 1), jnp.float32),
+            pltpu.VMEM((shards, components, count), jnp.float32),
             pltpu.VMEM((count, width), jnp.float32),
             dma((2,)),
             dma((groups + 2,)),

time: 132 us -> 133 us (level); the launches traced: 132 us -> 131 us
  no operation moved by 1% of the time
where the time goes in v2:
time: 133 us; the launch traced here: 131 us
  Pallas kernels  124 us (93%)
  matrix products  3.66 us (3%)
  local copies, waits for them, and re-layouts  2.23 us (2%)
    pallas_call x2, Pallas kernels, step(): pl.pallas_call(functools.partial(step_kernel, groups, shards), out_shape=...  124 us
    dot_general x3, matrix products, apply(): lax.dot_general(matrix, rows, dims, precision=lax.Precision.HIGHEST, pref...  3.41 us

profile of v2, /device:TPU:9, one launch (start us, length us, event | category | flops | bytes accessed | tf_op | source)
XLA Modules:
  0.0 130.5 jit_solution(391595143575797224)
XLA Ops:
  0.0 0.0 copy-start
  0.0 0.8 fusion.9
  0.8 0.1 convert_reduce_fusion.1
  0.9 0.0 copy-start.2
  0.9 0.1 convert_reduce_fusion
  1.0 0.6 copy-done.2
  1.6 0.0 copy-start.3
  1.6 0.7 copy-done.3
  2.3 0.1 copy.7.logw_ref
  2.3 0.2 fusion.4
  2.6 0.0 copy-done
  2.6 0.0 copy-start.1
  2.6 0.7 fusion.rows_ref
  3.3 0.1 copy-done.1
  3.4 63.0 %shard_map.46 = f32[256,1024]{1,0:T(8,128)S(1)} custom-call(f32[256,1024]{1,0:T(8,128)S(1)} %fusion.rows_ref, f32[16,1024]{1,0:T(8,128)S(1)} %copy-done.1, f32[16,1]{1,0:T(8,128)S(1)} %copy.7.logw_ref), custom_call_target="tpu_custom_call" | custom-call | tf_op jit(solution)/shard_map/pallas_call | solution.py:268
  66.5 1.0 fusion.10.rows_ref
  67.5 61.3 %shard_map.47 = f32[256,1024]{1,0:T(8,128)S(1)} custom-call(f32[256,1024]{1,0:T(8,128)S(1)} %fusion.10.rows_ref, f32[16,1024]{1,0:T(8,128)S(1)} %copy-done.1, f32[16,1]{1,0:T(8,128)S(1)} %copy.7.logw_ref), custom_call_target="tpu_custom_call" | custom-call | tf_op jit(solution)/shard_map/pallas_call | solution.py:268
  128.8 1.7 %fusion.3 = f32[256,1024]{1,0:T(8,128)} fusion(f32[256,1024]{1,0:T(8,128)S(1)} %shard_map.47, s32[256]{0:T(256)S(1)} %bitcast.12), kind=kOutput, calls=%fused_computation.10 | convolution fusion | flops 805371904 | bytes 2098176 | tf_op jit(solution)/shard_map/dot_general | solution.py:311
  (1 shorter events, 0.0 us)
Async XLA Ops:
  0.0 2.6 %copy-start = (f32[256,1024]{1,0:T(8,128)S(1)}, f32[256,1024]{1,0:T(8,128)}, u32[]{:S(2)}) copy-start(f32[256,1024]{1,0:T(8,128)} %param.4) | copy-start | bytes 3145732
  0.9 0.7 copy-start.2
  1.6 0.7 copy-start.3
  2.6 0.8 copy-start.1
